TPU v7x, 32 devices: a whole 2x2x4 slice. The times are simulated.
32 devices in a mesh: gy: 8 (over z, y), gz: 4 (over x, core).
Axes of the slice: x: 2, y: 2, z: 4, core: 2. Of those that a mesh axis runs over, the one named last changes fastest.
Arguments:
- tokens: bfloat16 [2, 64, 8, 8, 1024], P(None, None, 'gy', 'gz'), may hold values from -64 to 64
- w_qkv: bfloat16 [1024, 3072], P('gy'), may hold values from -2 to 2
- w_out: bfloat16 [1024, 1024], P('gy'), may hold values from -0.1875 to 0.1875
- bias_x: float32 [16, 127], replicated, may hold values from -4 to 4
- bias_y: float32 [16, 15], replicated, may hold values from -4 to 4
- bias_z: float32 [16, 15], replicated, may hold values from -4 to 4
Outputs:
- mixed: bfloat16 [2, 64, 8, 8, 1024], P(None, None, 'gy', 'gz')
All inputs are finite; a program needn't handle non-finite values.
Results may differ from a plain program's by a relative error of at most 0.0083.
Values may be sent and summed in bfloat16 or wider, within the bound.
A program may use at most 64 MiB of HBM per device.

v0:
```python
import functools

import jax
import jax.numpy as jnp
import numpy as np
from jax import lax
from jax.experimental import pallas as pl
from jax.experimental.pallas import tpu as pltpu
from jax.sharding import PartitionSpec as P

HEADS = 16
HEAD = 64


einsum_forms = {
    1: ("bxyzhs,bwyzhs->byzhxw", "byzhxw,bwyzhs->bxyzhs"),
    2: ("bxyzhs,bxwzhs->bxzhyw", "bxzhyw,bxwzhs->bxyzhs"),
    3: ("bxyzhs,bxywhs->bxyhzw", "bxyhzw,bxywhs->bxyzhs"),
}


def norm_rows(tokens):
    values = tokens.astype(jnp.float32)
    center = jnp.mean(values, axis=-1, keepdims=True)
    spread = jnp.mean((values - center) ** 2, axis=-1, keepdims=True)
    return ((values - center) * lax.rsqrt(spread + 1e-05)).astype(jnp.bfloat16)


def rel_bias(table):
    length = (table.shape[1] + 1) // 2
    offsets = (
        lax.broadcasted_iota(jnp.int32, (length, length), 0)
        - lax.broadcasted_iota(jnp.int32, (length, length), 1)
        + length
        - 1
    )
    lookup = (
        offsets[:, :, None] == lax.broadcasted_iota(jnp.int32, (1, 1, 2 * length - 1), 2)
    ).astype(jnp.float32)
    return jnp.einsum("hr,ijr->hij", table, lookup, precision=lax.Precision.HIGHEST)


def attend(qkv, table, axis):
    dims = qkv.shape
    features = dims[-1] // 3
    parts = qkv.reshape(dims[:-1] + (3, HEADS, HEAD))
    query = parts[..., 0, :, :]
    keys = parts[..., 1, :, :]
    values = parts[..., 2, :, :]
    score_form, mix_form = einsum_forms[axis]
    scores = jnp.einsum(score_form, query, keys, preferred_element_type=jnp.float32) * HEAD ** (
        -0.5
    ) + rel_bias(table)
    scores = scores - jnp.max(scores, axis=-1, keepdims=True)
    expo = jnp.exp(scores)
    weights = (expo / jnp.sum(expo, axis=-1, keepdims=True)).astype(jnp.bfloat16)
    mixed = jnp.einsum(mix_form, weights, values, preferred_element_type=jnp.float32)
    return mixed.reshape(dims[:-1] + (features,)).astype(jnp.bfloat16)


def return_y(result):
    return lax.all_to_all(result, "gy", split_axis=2, concat_axis=1, tiled=True)


def return_z(result):
    return lax.all_to_all(result, "gz", split_axis=3, concat_axis=1, tiled=True)


def shards(tokens, w_qkv, w_out, bias_x, bias_y, bias_z):
    samples, depth, rows_y, rows_z, features = tokens.shape
    normed = norm_rows(tokens)
    gathered = lax.all_gather(w_qkv, "gy", axis=0, tiled=True)

    def project(inputs):
        product = jnp.dot(
            inputs.reshape(-1, features), gathered, preferred_element_type=jnp.float32
        )
        return product.astype(jnp.bfloat16).reshape(inputs.shape[:-1] + (3 * features,))

    along_x = attend(project(normed), bias_x, 1)
    along_y = return_y(
        attend(
            project(lax.all_to_all(normed, "gy", split_axis=1, concat_axis=2, tiled=True)),
            bias_y,
            2,
        )
    )
    along_z = return_z(
        attend(
            project(lax.all_to_all(normed, "gz", split_axis=1, concat_axis=3, tiled=True)),
            bias_z,
            3,
        )
    )
    summed = along_x.astype(jnp.float32) + along_y.astype(jnp.float32) + along_z.astype(jnp.float32)
    summed = summed.astype(jnp.bfloat16).reshape(-1, features)
    residual = tokens.reshape(-1, features).astype(jnp.float32)
    result = residual + jnp.dot(
        summed, lax.all_gather(w_out, "gy", axis=0, tiled=True), preferred_element_type=jnp.float32
    )
    return result.astype(jnp.bfloat16).reshape(tokens.shape)


def device(**where):
    return {"device_id": where, "device_id_type": pl.DeviceIdType.MESH}


def greet(me_y, me_z, size_y, size_z):
    barrier = pltpu.get_barrier_semaphore()
    for step in range(1, size_y):
        pl.semaphore_signal(barrier, inc=1, **device(gy=lax.rem(me_y + step, size_y)))
    for step in range(1, size_z):
        pl.semaphore_signal(barrier, inc=1, **device(gz=lax.rem(me_z + step, size_z)))
    pl.semaphore_wait(barrier, size_y + size_z - 2)


def exchange(source, target, axis, me, size, send_sems, recv_sems):
    rows = source.shape[1] // size
    copies = []
    for step in range(1, size):
        peer = lax.rem(me + step, size)
        copies.append(
            pltpu.make_async_remote_copy(
                src_ref=source.at[:, pl.ds(pl.multiple_of(peer * rows, rows), rows), :],
                dst_ref=target.at[:, pl.ds(pl.multiple_of(me * rows, rows), rows), :],
                send_sem=send_sems.at[step - 1],
                recv_sem=recv_sems.at[step - 1],
                **device(**{axis: peer}),
            )
        )
    for copy in copies:
        copy.start()
    return copies


def keep_own(source, target, me, size):
    rows = source.shape[1] // size
    own = pl.ds(pl.multiple_of(me * rows, rows), rows)
    target[:, own, :] = source[:, own, :]


def line_places(rows, size_y, size_z, rows_z):
    row = np.arange(rows)
    part_y, part_z = rows // size_y, rows // size_z
    return (
        (row // rows_z, row % rows_z),
        (row // part_y, row % part_y),
        (row // part_z * rows_z + row % rows_z, row % part_z // rows_z),
    )


def offset_lookup(places, lengths, rows):
    parts, base = [], 0
    total = sum(2 * length - 1 for length in lengths)
    for (position, line), length in zip(places, lengths):
        lookup = np.zeros((total, 2 * rows), np.float32)
        first, second = np.nonzero(line[:, None] == line[None, :])
        entry = position[first] - position[second] + length - 1 + base
        lookup[entry, rows - 1 - first + second] = 1.0
        parts.append(lookup)
        base += 2 * length - 1
    return np.concatenate(parts, axis=1)


def fused_kernel(
    size_y, size_z, rows_z, tokens, weights, offsets, result,
    along, full, biases, mixed, back_y, back_z,
    y_send, y_recv, z_send, z_recv, up_send, up_recv, down_send, down_recv,
    side_send, side_recv, far_send, far_recv, core_send, core_recv, twin_send, twin_recv,
    ry_send, ry_recv, rz_send, rz_recv,
):
    me_y, me_z = lax.axis_index("gy"), lax.axis_index("gz")
    samples, rows, features = tokens.shape
    depth = weights.shape[1]
    half = depth // 2
    lone = half * 3 // 8
    held = half - lone
    levels = size_y // 2
    wide = 4 * HEAD
    groups = features // wide
    level, side, core = me_y // 2, lax.rem(me_y, 2), lax.rem(me_z, 2)
    flank = lax.rem(me_z // 2, 2)
    above, below = {"gy": me_y + 2}, {"gy": me_y - 2}
    beside = {"gy": level * 2 + 1 - side}
    twin = {"gz": me_z + 1 - 2 * core}
    far = {"gz": me_z + 2 - 4 * flank}

    values = tokens[...].astype(jnp.float32)
    center = jnp.mean(values, axis=-1, keepdims=True)
    spread = jnp.mean((values - center) ** 2, axis=-1, keepdims=True)
    along[0] = ((values - center) * lax.rsqrt(spread + 1e-05)).astype(jnp.bfloat16)

    greet(me_y, me_z, size_y, size_z)

    def columns_of(group):
        return pl.ds(pl.multiple_of(group * wide, wide), wide)

    def transfer(group, lev, sid, start, count, sends, recvs, slot, where, own=False):
        first = core * half + start
        cols = columns_of(group)
        block = full.at[
            :, pl.ds(pl.multiple_of((lev * 2 + sid) * depth + first, 8), count), cols
        ]
        source = block
        if own:
            source = weights.at[:, pl.ds(pl.multiple_of(first, 8), count), cols]
        return pltpu.make_async_remote_copy(
            src_ref=source, dst_ref=block, send_sem=sends.at[group, slot],
            recv_sem=recvs.at[group, slot], **device(**where),
        )

    mine = flank * lone

    def up(group, step, own=False):
        return transfer(group, level - step, side, mine, held, up_send, up_recv, step, above, own)

    def up_in(group, step):
        return transfer(group, level - 1 - step, side, mine, held, up_send, up_recv, step, above)

    def down(group, step, own=False):
        return transfer(group, level + step, side, mine, held, down_send, down_recv, step, below, own)

    def down_in(group, step):
        return transfer(group, level + 1 + step, side, mine, held, down_send, down_recv, step, below)

    def across(group, lev, own=False):
        return transfer(group, lev, side, mine, held, side_send, side_recv, lev, beside, own)

    def across_in(group, lev):
        return transfer(group, lev, 1 - side, mine, held, side_send, side_recv, lev, beside)

    def share(group, lev, sid):
        return transfer(
            group, lev, sid, mine, held, core_send, core_recv, lev * 2 + sid, twin
        )

    def to_far(group, lev, sid):
        return transfer(
            group, lev, sid, flank * held, lone, far_send, far_recv, lev * 2 + sid, far
        )

    def share_far(group, lev, sid):
        return transfer(
            group, lev, sid, (1 - flank) * held, lone,
            twin_send, twin_recv, lev * 2 + sid, twin,
        )

    def own_blocks(group):
        pl.when(level + 1 < levels)(lambda: up(group, 0, True).start())
        pl.when(level > 0)(lambda: down(group, 0, True).start())
        across(group, level, True).start()

    def spread_block(group, lev, sid):
        to_far(group, lev, sid).start()
        share(group, lev, sid).start()

    def chain(group, step):
        @pl.when(level - 1 - step >= 0)
        def _():
            up_in(group, step).wait_recv()
            pl.when(level + 1 < levels)(lambda: up(group, step + 1).start())
            across(group, level - 1 - step).start()
            spread_block(group, level - 1 - step, side)

        @pl.when(level + 1 + step < levels)
        def _():
            down_in(group, step).wait_recv()
            pl.when(level > 0)(lambda: down(group, step + 1).start())
            across(group, level + 1 + step).start()
            spread_block(group, level + 1 + step, side)

    def from_side(group, step):
        def arrived(lev):
            across_in(group, lev).wait_recv()
            spread_block(group, lev, 1 - side)

        if step == 0:
            arrived(level)
        else:
            pl.when(level - step >= 0)(lambda: arrived(level - step))
            pl.when(level + step < levels)(lambda: arrived(level + step))

    def each_block(act):
        act(level, 1 - side)
        for step in range(1, levels):
            for lev, there in ((level - step, level - step >= 0), (level + step, level + step < levels)):

                @pl.when(there)
                def _():
                    act(lev, side)
                    act(lev, 1 - side)

    def from_far(group):
        def act(lev, sid):
            to_far_in = transfer(
                group, lev, sid, (1 - flank) * held, lone,
                far_send, far_recv, lev * 2 + sid, far,
            )
            to_far_in.wait_recv()
            share_far(group, lev, sid).start()

        each_block(act)

    def complete(group):
        def act(lev, sid):
            transfer(
                group, lev, sid, mine, held, core_send, core_recv, lev * 2 + sid, twin
            ).wait_recv()
            share_far(group, lev, sid).wait_recv()

        each_block(act)

    def drain(group):
        pl.when(level + 1 < levels)(lambda: up(group, 0, True).wait_send())
        pl.when(level > 0)(lambda: down(group, 0, True).wait_send())
        across(group, level, True).wait_send()
        for step in range(1, levels):

            @pl.when(level - step >= 0)
            def _():
                pl.when(level + 1 < levels)(lambda: up(group, step).wait_send())
                across(group, level - step).wait_send()

            @pl.when(level + step < levels)
            def _():
                pl.when(level > 0)(lambda: down(group, step).wait_send())
                across(group, level + step).wait_send()

        def act(lev, sid):
            to_far(group, lev, sid).wait_send()
            share(group, lev, sid).wait_send()
            share_far(group, lev, sid).wait_send()

        each_block(act)

    own_blocks(0)
    sent_y = exchange(along.at[0], along.at[1], "gy", me_y, size_y, y_send, y_recv)
    sent_z = exchange(along.at[0], along.at[2], "gz", me_z, size_z, z_send, z_recv)
    for group in range(1, groups):
        own_blocks(group)
    full[:, pl.ds(pl.multiple_of(me_y * depth, depth), depth), :] = weights[...]
    keep_own(along.at[0], along.at[1], me_y, size_y)
    keep_own(along.at[0], along.at[2], me_z, size_z)

    row = lax.broadcasted_iota(jnp.int32, (rows, rows), 0)
    col = lax.broadcasted_iota(jnp.int32, (rows, rows), 1)
    lane = lax.broadcasted_iota(jnp.int32, (rows, 2 * HEAD), 1)
    part_y, part_z = rows // size_y, rows // size_z
    line_of = (
        lambda r: lax.rem(r, rows_z),
        lambda r: lax.rem(r, part_y),
        lambda r: lax.rem(r, part_z) // rows_z,
    )

    def fill_bias(group, carry):
        for axis in range(3):
            same = line_of[axis](row) == line_of[axis](col)
            for head in range(4):
                entry = offsets[group, head, axis * 2 * rows : (axis + 1) * 2 * rows]
                table = jnp.broadcast_to(entry[None, :], (rows, 2 * rows))
                table = pltpu.roll(table, rows + 1, 1, stride=1, stride_axis=0)
                biases[axis, group * 4 + head] = jnp.where(same, table[:, :rows], -1e30)
        return carry

    lax.fori_loop(0, groups, fill_bias, 0)

    hops = levels - 1
    waves = [
        [(wave - step, step) for step in range(hops) if 0 <= wave - step < groups]
        for wave in range(groups + hops - 1)
    ]

    def run(chosen):
        for wave in chosen:
            for group, step in wave:
                chain(group, step)

    run(waves[:hops])
    for step in range(levels):
        from_side(0, step)
    run(waves[hops : hops + 1])
    from_far(0)
    if groups > 1:
        for step in range(levels):
            from_side(1, step)
    run(waves[hops + 1 : -1])
    for copy in sent_y + sent_z:
        copy.wait()
    complete(0)

    def attend(group, axis, query, keys, contents):
        units = [
            (pair, sample, odd)
            for pair in range(wide // (2 * HEAD)) for sample in range(samples) for odd in range(2)
        ]

        def parts(pair, sample):
            first = (axis * samples + sample) * rows
            return slice(first, first + rows), slice(pair * 2 * HEAD, (pair + 1) * 2 * HEAD)

        scores, expos, totals, outs = {}, {}, {}, {}
        for unit in units:
            pair, sample, odd = unit
            part = parts(pair, sample)
            chosen = jnp.where(lane // HEAD == odd, query[part], 0)
            scores[unit] = lax.dot_general(
                chosen, keys[part], (((1,), (1,)), ((), ())), preferred_element_type=jnp.float32
            ) + biases[axis, group * 4 + pair * 2 + odd]
        for unit in units:
            expos[unit] = jnp.exp(scores[unit] - jnp.max(scores[unit], axis=-1, keepdims=True))
            totals[unit] = jnp.sum(expos[unit], axis=-1, keepdims=True)
        for unit in units:
            outs[unit] = jnp.dot(
                expos[unit].astype(jnp.bfloat16), contents[parts(*unit[:2])],
                preferred_element_type=jnp.float32,
            )
        for pair, sample, odd in units[::2]:
            place = pl.ds(pl.multiple_of(group * wide + pair * 2 * HEAD, 2 * HEAD), 2 * HEAD)
            even, other = (pair, sample, 0), (pair, sample, 1)
            mixed[axis, sample, :, place] = jnp.where(
                lane < HEAD, outs[even] * (1.0 / totals[even]), outs[other] * (1.0 / totals[other])
            ).astype(jnp.bfloat16)

    def returns(group):
        cols = columns_of(group)
        there = [
            (mixed.at[1], back_y, "gy", me_y, size_y, ry_send, ry_recv),
            (mixed.at[2], back_z, "gz", me_z, size_z, rz_send, rz_recv),
        ]
        copies = []
        for source, target, axis, me, size, sends, recvs in there:
            count = rows // size
            for step in range(1, size):
                peer = lax.rem(me + step, size)
                copies.append(
                    pltpu.make_async_remote_copy(
                        src_ref=source.at[:, pl.ds(pl.multiple_of(peer * count, count), count), cols],
                        dst_ref=target.at[:, pl.ds(pl.multiple_of(me * count, count), count), cols],
                        send_sem=sends.at[group, step - 1],
                        recv_sem=recvs.at[group, step - 1],
                        **device(**{axis: peer}),
                    )
                )
        return copies

    def group_step(group, carry):
        ahead, later = group + 1, group + 2
        flat = along[...].reshape(3 * samples * rows, features)
        cols = columns_of(group)

        def project(which):
            return jnp.dot(flat, full[which, :, cols], preferred_element_type=jnp.float32)

        def bring(chosen):
            @pl.when(later < groups)
            def _():
                for step in chosen:
                    from_side(later, step)

        if len(waves) > hops + 1:
            pl.when(group == 0)(lambda: run(waves[-1:]))
        pl.when(ahead < groups)(lambda: from_far(ahead))
        query = (project(0) * HEAD ** (-0.5)).astype(jnp.bfloat16)
        keys = project(1).astype(jnp.bfloat16)
        contents = project(2).astype(jnp.bfloat16)
        bring(range(levels - 2))
        attend(group, 1, query, keys, contents)
        bring(range(levels - 2, levels))
        attend(group, 2, query, keys, contents)
        copies = returns(group)
        for copy in copies[: size_y - 1]:
            copy.start()
        attend(group, 0, query, keys, contents)
        for copy in copies[size_y - 1 :]:
            copy.start()
        pl.when(ahead < groups)(lambda: complete(ahead))
        return carry

    lax.fori_loop(0, groups, group_step, 0)
    keep_own(mixed.at[1], back_y, me_y, size_y)
    keep_own(mixed.at[2], back_z, me_z, size_z)

    def finish(group, carry):
        drain(group)
        for copy in returns(group):
            copy.wait()
        return carry

    lax.fori_loop(0, groups, finish, 0)
    summed = mixed[0].astype(jnp.float32) + back_y[...].astype(jnp.float32)
    summed = (summed + back_z[...].astype(jnp.float32)).astype(jnp.bfloat16)
    summed = summed.reshape(-1, features)
    for first in range(0, features, wide):
        cols = slice(first, first + wide)
        product = jnp.dot(summed, full[3, :, cols], preferred_element_type=jnp.float32)
        residual = tokens[:, :, cols].astype(jnp.float32)
        result[:, :, cols] = (residual + product.reshape(residual.shape)).astype(jnp.bfloat16)


VMEM = pl.BlockSpec(memory_space=pltpu.VMEM)
DMA = pltpu.SemaphoreType.DMA


def fast_shards(size_y, size_z, tokens, w_qkv, w_out, bias_x, bias_y, bias_z):
    samples, depth, rows_y, rows_z, features = tokens.shape
    rows = depth * rows_y * rows_z
    levels = size_y // 2
    groups = features // (4 * HEAD)
    lengths = [(table.shape[1] + 1) // 2 for table in (bias_x, bias_y, bias_z)]
    lookup = offset_lookup(line_places(rows, size_y, size_z, rows_z), lengths, rows)
    offsets = jnp.dot(
        jnp.concatenate([bias_x, bias_y, bias_z], axis=1), lookup, precision=lax.Precision.HIGHEST
    )
    weights = jnp.stack([w_qkv[:, n * features : (n + 1) * features] for n in range(3)] + [w_out])
    block = (samples, rows, features)
    result = pl.pallas_call(
        functools.partial(fused_kernel, size_y, size_z, rows_z),
        out_shape=jax.ShapeDtypeStruct(block, jnp.bfloat16),
        in_specs=[VMEM, VMEM, VMEM],
        out_specs=VMEM,
        scratch_shapes=[
            pltpu.VMEM((3,) + block, jnp.bfloat16),
            pltpu.VMEM((4, features, features), jnp.bfloat16),
            pltpu.VMEM((3, HEADS, rows, rows), jnp.float32),
            pltpu.VMEM((3,) + block, jnp.bfloat16),
            pltpu.VMEM(block, jnp.bfloat16),
            pltpu.VMEM(block, jnp.bfloat16),
            DMA((size_y - 1,)), DMA((size_y - 1,)), DMA((size_z - 1,)), DMA((size_z - 1,)),
            DMA((groups, levels)), DMA((groups, levels)), DMA((groups, levels)), DMA((groups, levels)),
            DMA((groups, levels)), DMA((groups, levels)),
            DMA((groups, size_y)), DMA((groups, size_y)),
            DMA((groups, size_y)), DMA((groups, size_y)),
            DMA((groups, size_y)), DMA((groups, size_y)),
            DMA((groups, size_y - 1)), DMA((groups, size_y - 1)),
            DMA((groups, size_z - 1)), DMA((groups, size_z - 1)),
        ],
        compiler_params=pltpu.CompilerParams(collective_id=0, has_side_effects=True),
    )(tokens.reshape(block), weights, offsets.reshape(groups, 4, 6 * rows))
    return result.reshape(tokens.shape)


def body_for(size_y, size_z):
    def body(tokens, *parameters):
        _, depth, rows_y, rows_z, features = tokens.shape
        rows = depth * rows_y * rows_z
        whole_parts = size_y % 2 == 0 and size_z % 4 == 0 and rows == 2 * HEAD
        if whole_parts and rows_y == 1 and rows % (16 * size_y) == 0 and rows % (16 * size_z) == 0:
            return fast_shards(size_y, size_z, tokens, *parameters)
        return shards(tokens, *parameters)

    return body


def solution(mesh):
    placed = (P(None, None, "gy", "gz", None), P("gy", None), P("gy", None), P(), P(), P())
    return jax.shard_map(
        body_for(mesh.shape["gy"], mesh.shape["gz"]),
        mesh=mesh,
        in_specs=placed,
        out_specs=P(None, None, "gy", "gz", None),
        check_vma=False,
    )
```

profile of v0, /device:TPU:1, one launch (start us, length us, event | category | flops | bytes accessed | tf_op | source)
XLA Modules:
  0.0 84.9 jit_solution(1720898792185522966)
XLA Ops:
  0.0 0.0 copy-start
  0.0 0.0 copy-start.3
  0.0 1.2 %slice_bitcast_fusion.2 = (bf16[1,128,1024]{2,1,0:T(8,128)(2,1)S(1)}, bf16[1,128,1024]{2,1,0:T(8,128)(2,1)S(1)}, bf16[1,128,1024]{2,1,0:T(8,128)(2,1)S(1)}) fusion(bf16[128,3072]{1,0:T(8,128)(2,1)} %param.8), kind=kLoop, calls=%fused_computation.6 | loop fusion | bytes 1572864 | tf_op jit(solution)/shard_map/stack | solution.py:514
  1.2 0.0 copy-done.3
  1.2 0.0 copy-start.1
  1.2 1.1 %pad_maximum_fusion.weights = bf16[4,128,1024]{2,1,0:T(8,128)(2,1)} fusion(bf16[1,128,1024]{2,1,0:T(8,128)(2,1)S(1)} %bitcast.16, bf16[1,128,1024]{2,1,0:T(8,128)(2,1)S(1)} %get-tuple-element.6, bf16[1,128,1024]{2,1,0:T(8,128)(2,1)S(1)} %get-tuple-element.7, bf16[1,128,1024]{2,1,0:T(8,128)(2,1)S(1)} %get-tuple-element.5), kind=kLoop, calls=%fused_computation.3 | loop fusion | flops 1572864 | bytes 2097152 | tf_op jit(solution)/shard_map/stack | solution.py:514
  2.3 0.0 copy-done.1
  2.3 0.0 copy-start.2
  2.3 1.0 %reshape.9.tokens = bf16[2,128,1024]{2,1,0:T(8,128)(2,1)} reshape(bf16[2,64,1,2,1024]{4,3,2,1,0:T(2,128)(2,1)S(1)} %copy-done.1) | data formatting | bytes 1048576 | tf_op jit(solution)/shard_map/reshape | solution.py:538
  3.3 0.0 copy-done
  3.3 0.0 copy-done.2
  3.3 0.0 copy-start.5
  3.3 0.0 copy-start.6
  3.3 0.3 fusion.1
  3.7 0.5 copy-done.5
  4.1 0.0 copy-done.6
  4.1 0.0 copy-start.4
  4.1 0.0 copy-start.7
  4.1 0.2 convolution_add_fusion.1
  4.3 0.6 copy-done.4
  4.9 0.0 copy-done.7
  4.9 0.2 fusion
  5.1 0.6 reshape.10.offsets
  5.8 77.1 %shard_map.73 = bf16[2,128,1024]{2,1,0:T(8,128)(2,1)} custom-call(bf16[2,128,1024]{2,1,0:T(8,128)(2,1)} %reshape.9.tokens, bf16[4,128,1024]{2,1,0:T(8,128)(2,1)} %pad_maximum_fusion.weights, f32[4,4,768]{2,1,0:T(4,128)} %reshape.10.offsets), custom_call_target="tpu_custom_call" | custom-call | tf_op jit(solution)/shard_map/pallas_call | solution.py:516
  82.9 2.0 %reshape.11 = bf16[2,64,1,2,1024]{4,3,1,0,2:T(2,128)(2,1)} reshape(bf16[2,128,1024]{2,1,0:T(8,128)(2,1)} %shard_map.73) | data formatting | bytes 1048576 | tf_op jit(solution)/shard_map/reshape | solution.py:539
Async XLA Ops:
  0.0 3.3 %copy-start = (f32[16,127]{1,0:T(8,128)S(1)}, f32[16,127]{1,0:T(8,128)}, u32[]{:S(2)}) copy-start(f32[16,127]{1,0:T(8,128)} %param.10) | copy-start | bytes 24388
  0.0 1.2 %copy-start.3 = (bf16[128,1024]{1,0:T(8,128)(2,1)S(1)}, bf16[128,1024]{1,0:T(8,128)(2,1)}, u32[]{:S(2)}) copy-start(bf16[128,1024]{1,0:T(8,128)(2,1)} %param.9) | copy-start | bytes 786436
  1.2 1.1 %copy-start.1 = (bf16[2,64,1,2,1024]{4,3,2,1,0:T(2,128)(2,1)S(1)}, bf16[2,64,1,2,1024]{4,3,2,1,0:T(2,128)(2,1)}, u32[]{:S(2)}) copy-start(bf16[2,64,1,2,1024]{4,3,2,1,0:T(2,128)(2,1)} %param.7) | copy-start | bytes 1572868
  2.3 1.0 %copy-start.2 = (f32[127,768]{1,0:T(8,128)S(1)}, f32[127,768]{1,0:T(8,128)}, u32[]{:S(2)}) copy-start(f32[127,768]{1,0:T(8,128)} %constant.4) | copy-start | bytes 1170436
  3.3 0.8 copy-start.5
  3.3 0.8 copy-start.6
  4.1 0.8 copy-start.4
  4.1 0.8 copy-start.7
where the time goes:
time: 86.2 us; the launch traced here: 84.9 us
  Pallas kernels  77.1 us (89%)
  local copies, waits for them, and re-layouts  5.96 us (7%)
  other arithmetic  1.1 us (1%)
    pallas_call x1, Pallas kernels, fast_shards(): pl.pallas_call(functools.partial(fused_kernel, size_y, size_z, rows_z), o...  77.1 us
    reshape x1, local copies, waits for them, and re-layouts, fast_shards(): return result.reshape(tokens.shape)  2.03 us

commit v1 on v0

v1 whole, which is shorter than its diff:
```python
import functools

import jax
import jax.numpy as jnp
import numpy as np
from jax import lax
from jax.experimental import pallas as pl
from jax.experimental.pallas import tpu as pltpu
from jax.sharding import PartitionSpec as P

HEADS = 16
HEAD = 64


einsum_forms = {
    1: ("bxyzhs,bwyzhs->byzhxw", "byzhxw,bwyzhs->bxyzhs"),
    2: ("bxyzhs,bxwzhs->bxzhyw", "bxzhyw,bxwzhs->bxyzhs"),
    3: ("bxyzhs,bxywhs->bxyhzw", "bxyhzw,bxywhs->bxyzhs"),
}


def norm_rows(tokens):
    values = tokens.astype(jnp.float32)
    center = jnp.mean(values, axis=-1, keepdims=True)
    spread = jnp.mean((values - center) ** 2, axis=-1, keepdims=True)
    return ((values - center) * lax.rsqrt(spread + 1e-05)).astype(jnp.bfloat16)


def rel_bias(table):
    length = (table.shape[1] + 1) // 2
    offsets = (
        lax.broadcasted_iota(jnp.int32, (length, length), 0)
        - lax.broadcasted_iota(jnp.int32, (length, length), 1)
        + length
        - 1
    )
    lookup = (
        offsets[:, :, None] == lax.broadcasted_iota(jnp.int32, (1, 1, 2 * length - 1), 2)
    ).astype(jnp.float32)
    return jnp.einsum("hr,ijr->hij", table, lookup, precision=lax.Precision.HIGHEST)


def attend(qkv, table, axis):
    dims = qkv.shape
    features = dims[-1] // 3
    parts = qkv.reshape(dims[:-1] + (3, HEADS, HEAD))
    query = parts[..., 0, :, :]
    keys = parts[..., 1, :, :]
    values = parts[..., 2, :, :]
    score_form, mix_form = einsum_forms[axis]
    scores = jnp.einsum(score_form, query, keys, preferred_element_type=jnp.float32) * HEAD ** (
        -0.5
    ) + rel_bias(table)
    scores = scores - jnp.max(scores, axis=-1, keepdims=True)
    expo = jnp.exp(scores)
    weights = (expo / jnp.sum(expo, axis=-1, keepdims=True)).astype(jnp.bfloat16)
    mixed = jnp.einsum(mix_form, weights, values, preferred_element_type=jnp.float32)
    return mixed.reshape(dims[:-1] + (features,)).astype(jnp.bfloat16)


def return_y(result):
    return lax.all_to_all(result, "gy", split_axis=2, concat_axis=1, tiled=True)


def return_z(result):
    return lax.all_to_all(result, "gz", split_axis=3, concat_axis=1, tiled=True)


def shards(tokens, w_qkv, w_out, bias_x, bias_y, bias_z):
    samples, depth, rows_y, rows_z, features = tokens.shape
    normed = norm_rows(tokens)
    gathered = lax.all_gather(w_qkv, "gy", axis=0, tiled=True)

    def project(inputs):
        product = jnp.dot(
            inputs.reshape(-1, features), gathered, preferred_element_type=jnp.float32
        )
        return product.astype(jnp.bfloat16).reshape(inputs.shape[:-1] + (3 * features,))

    along_x = attend(project(normed), bias_x, 1)
    along_y = return_y(
        attend(
            project(lax.all_to_all(normed, "gy", split_axis=1, concat_axis=2, tiled=True)),
            bias_y,
            2,
        )
    )
    along_z = return_z(
        attend(
            project(lax.all_to_all(normed, "gz", split_axis=1, concat_axis=3, tiled=True)),
            bias_z,
            3,
        )
    )
    summed = along_x.astype(jnp.float32) + along_y.astype(jnp.float32) + along_z.astype(jnp.float32)
    summed = summed.astype(jnp.bfloat16).reshape(-1, features)
    residual = tokens.reshape(-1, features).astype(jnp.float32)
    result = residual + jnp.dot(
        summed, lax.all_gather(w_out, "gy", axis=0, tiled=True), preferred_element_type=jnp.float32
    )
    return result.astype(jnp.bfloat16).reshape(tokens.shape)


def device(**where):
    return {"device_id": where, "device_id_type": pl.DeviceIdType.MESH}


def line_places(rows, size_y, size_z, rows_z):
    row = np.arange(rows)
    part_y, part_z = rows // size_y, rows // size_z
    return (
        (row // rows_z, row % rows_z),
        (row // part_y, row % part_y),
        (row // part_z * rows_z + row % rows_z, row % part_z // rows_z),
    )


def offset_lookup(places, lengths, rows, width):
    lookup = np.zeros((len(lengths), width, 2 * rows), np.float32)
    for axis, ((position, line), length) in enumerate(zip(places, lengths)):
        first, second = np.nonzero(line[:, None] == line[None, :])
        entry = position[first] - position[second] + length - 1
        lookup[axis, entry, rows - 1 - first + second] = 1.0
    return lookup


def remote(source, target, sends, recvs, **where):
    return pltpu.make_async_remote_copy(
        src_ref=source, dst_ref=target, send_sem=sends, recv_sem=recvs, **device(**where)
    )


def heads_kernel(
    size_y, size_z, rows_z, tokens, w_qkv, w_out, bias_x, bias_y, bias_z, lookup, result,
    lines, wq, wo, padded, offsets, biases, qkv, mixed, ymixed, back, summed, parts, total,
    up_send, up_recv, down_send, down_recv, side_send, side_recv,
    y_send, y_recv, far_send, far_recv, twin_send, twin_recv, relay_send, relay_recv,
    o_send, o_recv, ry_send, ry_recv, ez_send, ez_recv,
):
    me_y, me_z = lax.axis_index("gy"), lax.axis_index("gz")
    samples, rows, features = tokens.shape
    depth = w_qkv.shape[0]
    wide = 2 * HEAD
    pairs = HEADS // (2 * size_z)
    slots = 3 * pairs
    items = slots + pairs
    levels = size_y // 2
    part_y, part_z = rows // size_y, rows // size_z
    level, side = me_y // 2, lax.rem(me_y, 2)
    core, flank = lax.rem(me_z, 2), me_z // 2
    above, below = {"gy": me_y + 2}, {"gy": me_y - 2}
    beside = {"gy": level * 2 + 1 - side}
    twin = me_z + 1 - 2 * core
    far = me_z + 2 - 4 * flank

    barrier = pltpu.get_barrier_semaphore()
    for step in range(1, size_y):
        pl.semaphore_signal(barrier, inc=1, **device(gy=lax.rem(me_y + step, size_y)))
    for step in range(1, size_z):
        pl.semaphore_signal(barrier, inc=1, **device(gz=lax.rem(me_z + step, size_z)))

    values = tokens[...].astype(jnp.float32)
    center = jnp.mean(values, axis=-1, keepdims=True)
    spread = jnp.mean((values - center) ** 2, axis=-1, keepdims=True)
    lines[0, me_z] = ((values - center) * lax.rsqrt(spread + 1e-05)).astype(jnp.bfloat16)

    pl.semaphore_wait(barrier, size_y + size_z - 2)

    def item_ref(item):
        return wq.at[item] if item < slots else wo.at[me_z * pairs + item - slots]

    def own_ref(item):
        if item < slots:
            start = item % 3 * features + (me_z * pairs + item // 3) * wide
            return w_qkv.at[:, pl.ds(pl.multiple_of(start, wide), wide)]
        start = (me_z * pairs + item - slots) * wide
        return w_out.at[:, pl.ds(pl.multiple_of(start, wide), wide)]

    def transfer(item, lev, sid, sends, recvs, slot, where, own=False):
        block = item_ref(item).at[pl.ds(pl.multiple_of((lev * 2 + sid) * depth, depth), depth)]
        source = own_ref(item) if own else block
        return remote(source, block, sends.at[item, slot], recvs.at[item, slot], **where)

    def up(item, step, own=False):
        return transfer(item, level - step, side, up_send, up_recv, step, above, own)

    def up_in(item, step):
        return transfer(item, level - 1 - step, side, up_send, up_recv, step, above)

    def down(item, step, own=False):
        return transfer(item, level + step, side, down_send, down_recv, step, below, own)

    def down_in(item, step):
        return transfer(item, level + 1 + step, side, down_send, down_recv, step, below)

    def across(item, lev, own=False):
        return transfer(item, lev, side, side_send, side_recv, lev, beside, own)

    def across_in(item, lev):
        return transfer(item, lev, 1 - side, side_send, side_recv, lev, beside)

    def own_blocks(item):
        pl.when(level + 1 < levels)(lambda: up(item, 0, True).start())
        pl.when(level > 0)(lambda: down(item, 0, True).start())
        across(item, level, True).start()

    def chain(item, step):
        @pl.when(level - 1 - step >= 0)
        def _():
            up_in(item, step).wait_recv()
            pl.when(level + 1 < levels)(lambda: up(item, step + 1).start())
            across(item, level - 1 - step).start()

        @pl.when(level + 1 + step < levels)
        def _():
            down_in(item, step).wait_recv()
            pl.when(level > 0)(lambda: down(item, step + 1).start())
            across(item, level + 1 + step).start()

    def chains(first, last):
        hops = levels - 1
        for wave in range(first, last + hops - 1):
            for step in range(hops):
                if first <= wave - step < last:
                    chain(wave - step, step)

    def from_side(item):
        for lev in range(levels):
            across_in(item, lev).wait_recv()

    def drain(item):
        pl.when(level + 1 < levels)(lambda: up(item, 0, True).wait_send())
        pl.when(level > 0)(lambda: down(item, 0, True).wait_send())
        across(item, level, True).wait_send()
        for step in range(1, levels):

            @pl.when(level - step >= 0)
            def _():
                pl.when(level + 1 < levels)(lambda: up(item, step).wait_send())
                across(item, level - step).wait_send()

            @pl.when(level + step < levels)
            def _():
                pl.when(level > 0)(lambda: down(item, step).wait_send())
                across(item, level + step).wait_send()

    pieces = samples + size_y

    def piece_of(index, block):
        if index < samples:
            return lines.at[0, block, index]
        peer = lax.rem(me_y + size_y - (index - samples), size_y)
        return lines.at[1, block, :, pl.ds(pl.multiple_of(peer * part_y, part_y), part_y), :]

    def to_far(index, block=me_z):
        ref = piece_of(index, block)
        return remote(ref, ref, far_send.at[index], far_recv.at[index], gz=far)

    def to_twin(index, block=me_z):
        ref = piece_of(index, block)
        return remote(ref, ref, twin_send.at[index], twin_recv.at[index], gz=twin)

    def relay(index, block=far):
        ref = piece_of(index, block)
        return remote(ref, ref, relay_send.at[index], relay_recv.at[index], gz=twin)

    def spread_piece(index):
        to_far(index).start()
        to_twin(index).start()

    def pass_on(index):
        to_far(index, far).wait_recv()
        relay(index).start()

    def exchange(step):
        peer = lax.rem(me_y + step, size_y)
        return remote(
            lines.at[0, me_z, :, pl.ds(pl.multiple_of(peer * part_y, part_y), part_y), :],
            lines.at[1, me_z, :, pl.ds(pl.multiple_of(me_y * part_y, part_y), part_y), :],
            y_send.at[step - 1], y_recv.at[step - 1], gy=peer,
        )

    def exchange_in(step):
        exchange(step).wait_recv()
        spread_piece(samples + step)

    def share_out(slot, block, where):
        ref = wo.at[pl.ds(block * pairs, pairs)]
        return remote(ref, ref, o_send.at[slot], o_recv.at[slot], gz=where)

    def returns(pair):
        copies = []
        for step in range(1, size_y):
            peer = lax.rem(me_y + step, size_y)
            copies.append(
                remote(
                    ymixed.at[pair, peer], back.at[pair, me_y],
                    ry_send.at[pair, step - 1], ry_recv.at[pair, step - 1], gy=peer,
                )
            )
        return copies

    def sums_out(pair):
        copies = []
        for step in range(1, size_z):
            peer = lax.rem(me_z + step, size_z)
            copies.append(
                remote(
                    summed.at[pair, peer], parts.at[pair, me_z],
                    ez_send.at[pair, step - 1], ez_recv.at[pair, step - 1], gz=peer,
                )
            )
        return copies

    row = lax.broadcasted_iota(jnp.int32, (rows, rows), 0)
    col = lax.broadcasted_iota(jnp.int32, (rows, rows), 1)
    lane = lax.broadcasted_iota(jnp.int32, (rows, wide), 1)
    line_of = (
        lambda r: lax.rem(r, rows_z),
        lambda r: lax.rem(r, part_y),
        lambda r: lax.rem(r, part_z) // rows_z,
    )

    def own_weights():
        mine = pl.ds(pl.multiple_of(me_y * depth, depth), depth)
        for item in range(items):
            item_ref(item)[mine, :] = own_ref(item)[...]

    def bias_tables():
        padded[...] = jnp.zeros(padded.shape, jnp.float32)
        for axis, table in enumerate((bias_x, bias_y, bias_z)):
            padded[axis, :, : table.shape[1]] = table[...]
            offsets[axis] = jnp.dot(
                padded[axis], lookup[axis],
                precision=lax.Precision.HIGHEST, preferred_element_type=jnp.float32,
            )

        def fill(head, carry):
            for axis in range(3):
                same = line_of[axis](row) == line_of[axis](col)
                entry = offsets[axis, pl.ds(me_z * 2 * pairs + head, 1), :]
                table = jnp.broadcast_to(entry, (rows, 2 * rows))
                table = pltpu.roll(table, rows + 1, 1, stride=1, stride_axis=0)
                biases[axis, head] = jnp.where(same, table[:, :rows], -1e30)
            return carry

        lax.fori_loop(0, 2 * pairs, fill, 0)

    def project(group, chunk, where):
        blocks = pl.ds(pl.multiple_of(where * 2, 2), 2)
        flat = lines[group, blocks].reshape(2 * samples * rows, features)
        both = jnp.concatenate([wq[2 * chunk], wq[2 * chunk + 1]], axis=1)
        product = jnp.dot(flat, both, preferred_element_type=jnp.float32)
        for half in range(2):
            item = 2 * chunk + half
            piece = product[:, half * wide : (half + 1) * wide]
            if item % 3 == 0:
                piece = piece * HEAD ** (-0.5)
            qkv[group, item, blocks] = piece.astype(jnp.bfloat16).reshape(2, samples, rows, wide)

    def attend(axis, pair, blocks):
        units = [(block, odd) for block in range(len(blocks)) for odd in range(2)]
        scores, expos, totals, outs = {}, {}, {}, {}
        for unit in units:
            block, odd = unit
            query, keys, _ = blocks[block]
            chosen = jnp.where(lane // HEAD == odd, query, 0)
            scores[unit] = lax.dot_general(
                chosen, keys, (((1,), (1,)), ((), ())), preferred_element_type=jnp.float32
            ) + biases[axis, pair * 2 + odd]
        for unit in units:
            expos[unit] = jnp.exp(scores[unit] - jnp.max(scores[unit], axis=-1, keepdims=True))
            totals[unit] = jnp.sum(expos[unit], axis=-1, keepdims=True)
        for unit in units:
            outs[unit] = jnp.dot(
                expos[unit].astype(jnp.bfloat16), blocks[unit[0]][2],
                preferred_element_type=jnp.float32,
            )
        return [
            jnp.where(
                lane < HEAD,
                outs[block, 0] * (1.0 / totals[block, 0]),
                outs[block, 1] * (1.0 / totals[block, 1]),
            ).astype(jnp.bfloat16)
            for block in range(len(blocks))
        ]

    def along_x(pair):
        def body(block, carry):
            blocks = [
                [qkv[0, pair * 3 + m, block, sample] for m in range(3)] for sample in range(samples)
            ]
            for sample, out in enumerate(attend(0, pair, blocks)):
                mixed[0, pair, block, sample] = out
            return carry

        lax.fori_loop(0, size_z, body, 0)

    def along_z(pair):
        def body(index, carry):
            some = pl.ds(pl.multiple_of(index * part_z, part_z), part_z)
            blocks = [
                [
                    jnp.concatenate(
                        [qkv[0, pair * 3 + m, z, sample, some, :] for z in range(size_z)], axis=0
                    )
                    for m in range(3)
                ]
                for sample in range(samples)
            ]
            for sample, out in enumerate(attend(2, pair, blocks)):
                for z in range(size_z):
                    mixed[1, pair, z, sample, some, :] = out[z * part_z : (z + 1) * part_z]
            return carry

        lax.fori_loop(0, size_z, body, 0)

    def along_y(pair):
        def body(block, carry):
            blocks = [
                [qkv[1, pair * 3 + m, block, sample] for m in range(3)] for sample in range(samples)
            ]
            for sample, out in enumerate(attend(1, pair, blocks)):
                for y in range(size_y):
                    ymixed[pair, y, block * samples + sample] = out[y * part_y : (y + 1) * part_y]
            return carry

        lax.fori_loop(0, size_z, body, 0)

    def add_up(pair):
        def body(block, carry):
            for sample in range(samples):
                there = jnp.concatenate(
                    [back[pair, y, block * samples + sample] for y in range(size_y)], axis=0
                )
                value = mixed[0, pair, block, sample].astype(jnp.float32) + there.astype(jnp.float32)
                value = value + mixed[1, pair, block, sample].astype(jnp.float32)
                summed[pair, block, sample] = value.astype(jnp.bfloat16)
            return carry

        for copy in returns(pair):
            copy.wait_recv()
        back[pair, me_y] = ymixed[pair, me_y]
        lax.fori_loop(0, size_z, body, 0)
        for copy in sums_out(pair):
            copy.start()
        parts[pair, me_z] = summed[pair, me_z]

    def output(pair):
        for copy in sums_out(pair):
            copy.wait_recv()
        left = jnp.concatenate(
            [parts[pair, z].reshape(samples * rows, wide) for z in range(size_z)], axis=1
        )
        for block in range(0, features // wide, 2):
            right = jnp.concatenate(
                [
                    jnp.concatenate(
                        [
                            wo[block + n, (z * pairs + pair) * wide : (z * pairs + pair + 1) * wide]
                            for z in range(size_z)
                        ],
                        axis=0,
                    )
                    for n in range(2)
                ],
                axis=1,
            )
            product = jnp.dot(left, right, preferred_element_type=jnp.float32)
            cols = slice(block * wide, (block + 2) * wide)
            if pair > 0:
                product = product + total[:, cols]
            if pair < pairs - 1:
                total[:, cols] = product
            else:
                residual = tokens[:, :, cols].astype(jnp.float32)
                result[:, :, cols] = (residual + product.reshape(residual.shape)).astype(jnp.bfloat16)

    early = 4
    for item in range(early):
        own_blocks(item)
    for sample in range(samples):
        spread_piece(sample)
    own_weights()
    lines[1, me_z, :, pl.ds(pl.multiple_of(me_y * part_y, part_y), part_y), :] = lines[
        0, me_z, :, pl.ds(pl.multiple_of(me_y * part_y, part_y), part_y), :
    ]
    bias_tables()
    chains(0, early)
    for step in range(1, size_y):
        exchange(step).start()
    spread_piece(samples)
    for item in range(early, items):
        own_blocks(item)
    pass_on(0)
    for item in range(2):
        from_side(item)
    for sample in range(samples):
        to_twin(sample, twin).wait_recv()
    project(0, 0, flank)
    for item in range(2, 4):
        from_side(item)
    project(0, 1, flank)
    pass_on(1)
    for step in range(1, 4):
        exchange_in(step)
    for sample in range(samples):
        relay(sample).wait_recv()
    project(0, 0, 1 - flank)
    project(0, 1, 1 - flank)
    along_x(0)
    for step in range(4, size_y):
        exchange_in(step)
    chains(early, items)
    along_z(0)
    for step in range(size_y):
        pass_on(samples + step)
    for step in range(size_y):
        to_twin(samples + step, twin).wait_recv()
    for item in range(slots, items):
        from_side(item)
    share_out(0, me_z, far).start()
    share_out(1, me_z, twin).start()
    project(1, 0, flank)
    project(1, 1, flank)
    for step in range(size_y):
        relay(samples + step).wait_recv()
    project(1, 0, 1 - flank)
    project(1, 1, 1 - flank)
    along_y(0)
    for copy in returns(0):
        copy.start()
    for item in range(early, slots):
        from_side(item)
    project(1, 2, flank)
    project(1, 2, 1 - flank)
    along_y(1)
    for copy in returns(1):
        copy.start()
    project(0, 2, flank)
    project(0, 2, 1 - flank)
    along_x(1)
    add_up(0)
    along_z(1)
    share_out(0, far, far).wait_recv()
    share_out(2, far, twin).start()
    add_up(1)
    share_out(1, twin, twin).wait_recv()
    share_out(2, 0, twin).wait_recv()
    output(0)
    output(1)
    for item in range(items):
        drain(item)
    for index in range(pieces):
        to_far(index).wait_send()
        to_twin(index).wait_send()
        relay(index).wait_send()
    for step in range(1, size_y):
        exchange(step).wait_send()
    for slot in range(3):
        share_out(slot, me_z, twin).wait_send()
    for pair in range(pairs):
        for copy in returns(pair) + sums_out(pair):
            copy.wait_send()


VMEM = pl.BlockSpec(memory_space=pltpu.VMEM)
DMA = pltpu.SemaphoreType.DMA


def fast_shards(size_y, size_z, tokens, w_qkv, w_out, bias_x, bias_y, bias_z):
    samples, depth, rows_y, rows_z, features = tokens.shape
    rows = depth * rows_y * rows_z
    levels = size_y // 2
    wide = 2 * HEAD
    pairs = HEADS // (2 * size_z)
    items = 4 * pairs
    pieces = samples + size_y
    lengths = [(table.shape[1] + 1) // 2 for table in (bias_x, bias_y, bias_z)]
    width = -(-max(2 * length - 1 for length in lengths) // 128) * 128
    lookup = offset_lookup(line_places(rows, size_y, size_z, rows_z), lengths, rows, width)
    block = (samples, rows, features)
    piled = (pairs, size_z, samples, rows, wide)
    sliced = (pairs, size_y, size_z * samples, rows // size_y, wide)
    result = pl.pallas_call(
        functools.partial(heads_kernel, size_y, size_z, rows_z),
        out_shape=jax.ShapeDtypeStruct(block, jnp.bfloat16),
        in_specs=[VMEM] * 7,
        out_specs=VMEM,
        scratch_shapes=[
            pltpu.VMEM((2, size_z) + block, jnp.bfloat16),
            pltpu.VMEM((3 * pairs, features, wide), jnp.bfloat16),
            pltpu.VMEM((features // wide, features, wide), jnp.bfloat16),
            pltpu.VMEM((3, HEADS, width), jnp.float32),
            pltpu.VMEM((3, HEADS, 2 * rows), jnp.float32),
            pltpu.VMEM((3, 2 * pairs, rows, rows), jnp.float32),
            pltpu.VMEM((2, 3 * pairs, size_z, samples, rows, wide), jnp.bfloat16),
            pltpu.VMEM((2,) + piled, jnp.bfloat16),
            pltpu.VMEM(sliced, jnp.bfloat16),
            pltpu.VMEM(sliced, jnp.bfloat16),
            pltpu.VMEM(piled, jnp.bfloat16),
            pltpu.VMEM(piled, jnp.bfloat16),
            pltpu.VMEM((samples * rows, features), jnp.float32),
        ]
        + [DMA((items, levels))] * 6
        + [DMA((size_y - 1,))] * 2
        + [DMA((pieces,))] * 6
        + [DMA((3,))] * 2
        + [DMA((pairs, size_y - 1))] * 2
        + [DMA((pairs, size_z - 1))] * 2,
        compiler_params=pltpu.CompilerParams(collective_id=0, has_side_effects=True),
    )(tokens.reshape(block), w_qkv, w_out, bias_x, bias_y, bias_z, jnp.asarray(lookup))
    return result.reshape(tokens.shape)


def body_for(size_y, size_z):
    def body(tokens, *parameters):
        _, depth, rows_y, rows_z, features = tokens.shape
        rows = depth * rows_y * rows_z
        fits = size_y % 2 == 0 and size_z == 4 and HEADS % (4 * size_z) == 0 and rows == 2 * HEAD
        if fits and rows_y == 1 and rows % (16 * size_y) == 0 and rows % (16 * size_z) == 0:
            return fast_shards(size_y, size_z, tokens, *parameters)
        return shards(tokens, *parameters)

    return body


def solution(mesh):
    placed = (P(None, None, "gy", "gz", None), P("gy", None), P("gy", None), P(), P(), P())
    return jax.shard_map(
        body_for(mesh.shape["gy"], mesh.shape["gz"]),
        mesh=mesh,
        in_specs=placed,
        out_specs=P(None, None, "gy", "gz", None),
        check_vma=False,
    )
```

time: 86.2 us -> 68.1 us (0.79)
  Pallas kernels: 77.1 us -> 63 us
  local copies, waits for them, and re-layouts: 5.96 us -> 4.07 us
  other arithmetic: 1.1 us -> 0 us
    pallas_call x1, Pallas kernels: 77.1 us -> 63 us  [fast_shards(): pl.pallas_call(functools.partial(heads_kernel, size_y, size_z, rows_z), o...]
    another operation x1 -> x0, local copies, waits for them, and re-layouts: 1.2 us -> none  [fast_shards(): jnp.stack([w_qkv[:, n * features:(n + 1) * features] for n in range(3)] +...]
    another operation x1 -> x0, other arithmetic: 1.1 us -> none  [fast_shards(): jnp.stack([w_qkv[:, n * features:(n + 1) * features] for n in range(3)] +...]
    unnamed x16 -> x0, local copies, waits for them, and re-layouts: 1.09 us -> none
    reshape x1, local copies, waits for them, and re-layouts: 0.99 us -> 2.03 us  [fast_shards(): tokens.reshape(block)]
where the time goes in v1:
time: 68.1 us; the launch traced here: 67.1 us
  Pallas kernels  63 us (93%)
  local copies, waits for them, and re-layouts  4.07 us (6%)
    pallas_call x1, Pallas kernels, fast_shards(): pl.pallas_call(functools.partial(heads_kernel, size_y, size_z, rows_z), o...  63 us
    reshape x1, local copies, waits for them, and re-layouts, fast_shards(): return result.reshape(tokens.shape)  2.03 us
    reshape x1, local copies, waits for them, and re-layouts, fast_shards(): tokens.reshape(block)  2.03 us

profile of v1, /device:TPU:1, one launch (start us, length us, event | category | flops | bytes accessed | tf_op | source)
XLA Modules:
  0.0 67.1 jit_solution(4415128423424969621)
XLA Ops:
  0.0 2.0 %reshape.6.tokens = bf16[2,128,1024]{2,1,0:T(8,128)(2,1)} reshape(bf16[2,64,1,2,1024]{4,3,2,1,0:T(2,128)(2,1)} %param.7) | data formatting | bytes 1048576 | tf_op jit(solution)/shard_map/reshape | solution.py:612
  2.0 63.0 %shard_map.73 = bf16[2,128,1024]{2,1,0:T(8,128)(2,1)} custom-call(bf16[2,128,1024]{2,1,0:T(8,128)(2,1)} %reshape.6.tokens, bf16[128,3072]{1,0:T(8,128)(2,1)} %w_qkv.1, bf16[128,1024]{1,0:T(8,128)(2,1)} %w_out.1, f32[16,127]{1,0:T(8,128)} %bias_x.1, f32[16,15]{1,0:T(8,128)} %bias_y.1, f32[16,15]{1,0:T(8,128)} %bias_z.1, f32[3,128,256]{2,1,0:T(8,128)} %constant.2.clone.lookup), custom_call_target="tpu_custom_call" | custom-call | tf_op jit(solution)/shard_map/pallas_call | solution.py:585
  65.1 2.0 %reshape.7 = bf16[2,64,1,2,1024]{4,3,1,0,2:T(2,128)(2,1)} reshape(bf16[2,128,1024]{2,1,0:T(8,128)(2,1)} %shard_map.73) | data formatting | bytes 1048576 | tf_op jit(solution)/shard_map/reshape | solution.py:613

commit v2 on v1

--- a/solution.py
+++ b/solution.py
@@ -131,14 +131,15 @@
 
 
 def heads_kernel(
-    size_y, size_z, rows_z, tokens, w_qkv, w_out, bias_x, bias_y, bias_z, lookup, result,
-    lines, wq, wo, padded, offsets, biases, qkv, mixed, ymixed, back, summed, parts, total,
+    size_y, size_z, tokens_in, w_qkv, w_out, bias_x_in, bias_y_in, bias_z_in, lookup_in, result,
+    tokens, bias_x, bias_y, bias_z, lookup, in_sem, own_sem, lines, wq, wo, padded, offsets, biases, qkv, mixed, ymixed, back, summed, parts, total,
     up_send, up_recv, down_send, down_recv, side_send, side_recv,
     y_send, y_recv, far_send, far_recv, twin_send, twin_recv, relay_send, relay_recv,
-    o_send, o_recv, ry_send, ry_recv, ez_send, ez_recv,
+    o_send, o_recv, of_send, of_recv, ry_send, ry_recv, ez_send, ez_recv,
 ):
     me_y, me_z = lax.axis_index("gy"), lax.axis_index("gz")
-    samples, rows, features = tokens.shape
+    samples, length, rows_z, features = tokens.shape
+    rows = length * rows_z
     depth = w_qkv.shape[0]
     wide = 2 * HEAD
     pairs = HEADS // (2 * size_z)
@@ -153,18 +154,31 @@
     twin = me_z + 1 - 2 * core
     far = me_z + 2 - 4 * flank
 
+    inputs = [
+        pltpu.make_async_copy(source, target, in_sem.at[index])
+        for index, (source, target) in enumerate(
+            (
+                (tokens_in, tokens), (bias_x_in, bias_x), (bias_y_in, bias_y),
+                (bias_z_in, bias_z), (lookup_in, lookup),
+            )
+        )
+    ]
+    for copy in inputs:
+        copy.start()
+
     barrier = pltpu.get_barrier_semaphore()
-    for step in range(1, size_y):
-        pl.semaphore_signal(barrier, inc=1, **device(gy=lax.rem(me_y + step, size_y)))
-    for step in range(1, size_z):
-        pl.semaphore_signal(barrier, inc=1, **device(gz=lax.rem(me_z + step, size_z)))
-
-    values = tokens[...].astype(jnp.float32)
-    center = jnp.mean(values, axis=-1, keepdims=True)
-    spread = jnp.mean((values - center) ** 2, axis=-1, keepdims=True)
-    lines[0, me_z] = ((values - center) * lax.rsqrt(spread + 1e-05)).astype(jnp.bfloat16)
-
-    pl.semaphore_wait(barrier, size_y + size_z - 2)
+    for dist in (1, 2):
+        pl.when(level + dist < levels)(
+            lambda: pl.semaphore_signal(barrier, inc=1, **device(gy=me_y + 2 * dist))
+        )
+        pl.when(level - dist >= 0)(
+            lambda: pl.semaphore_signal(barrier, inc=1, **device(gy=me_y - 2 * dist))
+        )
+    pl.semaphore_signal(barrier, inc=1, **device(**beside))
+    pl.semaphore_signal(barrier, inc=1, **device(gz=twin))
+    pl.semaphore_signal(barrier, inc=1, **device(gz=far))
+    near = jnp.minimum(level, 2) + jnp.minimum(levels - 1 - level, 2)
+    pl.semaphore_wait(barrier, near + 3)
 
     def item_ref(item):
         return wq.at[item] if item < slots else wo.at[me_z * pairs + item - slots]
@@ -199,10 +213,21 @@
     def across_in(item, lev):
         return transfer(item, lev, 1 - side, side_send, side_recv, lev, beside)
 
+    def far_block(item, lev, sid, gz, own=False):
+        part, index = item - slots, lev * 2 + sid
+        ref = wo.at[gz * pairs + part].at[pl.ds(pl.multiple_of(index * depth, depth), depth)]
+        source = own_ref(item) if own else ref
+        return remote(source, ref, of_send.at[part, index], of_recv.at[part, index], gz=far)
+
+    def block_out(item, lev, sid, own=False):
+        if item >= slots:
+            far_block(item, lev, sid, me_z, own).start()
+
     def own_blocks(item):
         pl.when(level + 1 < levels)(lambda: up(item, 0, True).start())
         pl.when(level > 0)(lambda: down(item, 0, True).start())
         across(item, level, True).start()
+        block_out(item, level, side, True)
 
     def chain(item, step):
         @pl.when(level - 1 - step >= 0)
@@ -210,23 +235,75 @@
             up_in(item, step).wait_recv()
             pl.when(level + 1 < levels)(lambda: up(item, step + 1).start())
             across(item, level - 1 - step).start()
+            block_out(item, level - 1 - step, side)
 
         @pl.when(level + 1 + step < levels)
         def _():
             down_in(item, step).wait_recv()
             pl.when(level > 0)(lambda: down(item, step + 1).start())
             across(item, level + 1 + step).start()
-
-    def chains(first, last):
-        hops = levels - 1
-        for wave in range(first, last + hops - 1):
-            for step in range(hops):
-                if first <= wave - step < last:
-                    chain(wave - step, step)
+            block_out(item, level + 1 + step, side)
+
+    def reach(item, dist, rise, passed=False):
+        sends, recvs = (up_send, up_recv) if rise else (down_send, down_recv)
+        sign = 1 if rise else -1
+        if passed:
+            return transfer(item, level - 2 * sign, side, sends, recvs, 2, {"gy": me_y + 2 * sign})
+        return transfer(
+            item, level, side, sends, recvs, dist - 1, {"gy": me_y + 2 * sign * dist}, True
+        )
+
+    def direct(item):
+        across(item, level, True).start()
+        for dist in (1, 2):
+            pl.when(level + dist < levels)(lambda: reach(item, dist, True).start())
+            pl.when(level - dist >= 0)(lambda: reach(item, dist, False).start())
+        block_out(item, level, side, True)
+
+    def arrive(item, dist):
+        @pl.when(level - dist >= 0)
+        def _():
+            reach(item, dist, True, dist == 3).wait_recv()
+            if dist == 2:
+                pl.when(level + 1 < levels)(lambda: reach(item, 3, True, True).start())
+            across(item, level - dist).start()
+            block_out(item, level - dist, side)
+
+        @pl.when(level + dist < levels)
+        def _():
+            reach(item, dist, False, dist == 3).wait_recv()
+            if dist == 2:
+                pl.when(level > 0)(lambda: reach(item, 3, False, True).start())
+            across(item, level + dist).start()
+            block_out(item, level + dist, side)
+
+    def drain_direct(item):
+        across(item, level, True).wait_send()
+        for dist in range(1, levels):
+
+            @pl.when(level + dist < levels)
+            def _():
+                if dist < 3:
+                    reach(item, dist, True).wait_send()
+                across(item, level + dist).wait_send()
+
+            @pl.when(level - dist >= 0)
+            def _():
+                if dist < 3:
+                    reach(item, dist, False).wait_send()
+                across(item, level - dist).wait_send()
+
+        pl.when(jnp.logical_and(level >= 2, level + 1 < levels))(
+            lambda: reach(item, 3, True, True).wait_send()
+        )
+        pl.when(jnp.logical_and(level + 2 < levels, level > 0))(
+            lambda: reach(item, 3, False, True).wait_send()
+        )
 
     def from_side(item):
         for lev in range(levels):
             across_in(item, lev).wait_recv()
+            block_out(item, lev, 1 - side)
 
     def drain(item):
         pl.when(level + 1 < levels)(lambda: up(item, 0, True).wait_send())
@@ -284,33 +361,52 @@
         exchange(step).wait_recv()
         spread_piece(samples + step)
 
-    def share_out(slot, block, where):
-        ref = wo.at[pl.ds(block * pairs, pairs)]
-        return remote(ref, ref, o_send.at[slot], o_recv.at[slot], gz=where)
-
-    def returns(pair):
+    def share_out(slot, part, block):
+        ref = wo.at[block * pairs + part]
+        return remote(ref, ref, o_send.at[slot, part], o_recv.at[slot, part], gz=twin)
+
+    def share(part):
+        from_side(slots + part)
+        share_out(0, part, me_z).start()
+
+    def relay_share(part):
+        for index in range(size_y):
+            far_block(slots + part, 0, index, far).wait_recv()
+        share_out(1, part, far).start()
+
+    def shared(part):
+        share_out(0, part, twin).wait_recv()
+        share_out(1, part, far).wait_recv()
+
+    def returns(pair, where):
+        some = pl.ds(pl.multiple_of(where * 2 * samples, 2 * samples), 2 * samples)
+        there = jnp.where(where == flank, 0, 1)
         copies = []
         for step in range(1, size_y):
             peer = lax.rem(me_y + step, size_y)
             copies.append(
                 remote(
-                    ymixed.at[pair, peer], back.at[pair, me_y],
-                    ry_send.at[pair, step - 1], ry_recv.at[pair, step - 1], gy=peer,
+                    ymixed.at[pair, peer, some], back.at[pair, me_y, some],
+                    ry_send.at[pair, there, step - 1], ry_recv.at[pair, there, step - 1], gy=peer,
                 )
             )
         return copies
 
-    def sums_out(pair):
-        copies = []
-        for step in range(1, size_z):
-            peer = lax.rem(me_z + step, size_z)
-            copies.append(
-                remote(
-                    summed.at[pair, peer], parts.at[pair, me_z],
-                    ez_send.at[pair, step - 1], ez_recv.at[pair, step - 1], gz=peer,
-                )
-            )
-        return copies
+    def give_back(pair, where):
+        along_y(pair, where)
+        for copy in returns(pair, where):
+            copy.start()
+
+    def sum_out(pair, peer, slot):
+        return remote(
+            summed.at[pair, peer], parts.at[pair, me_z],
+            ez_send.at[pair, slot], ez_recv.at[pair, slot], gz=peer,
+        )
+
+    def sums_out(pair, where):
+        if where is flank:
+            return [sum_out(pair, twin, 0)]
+        return [sum_out(pair, far, 1), sum_out(pair, far + twin - me_z, 2)]
 
     row = lax.broadcasted_iota(jnp.int32, (rows, rows), 0)
     col = lax.broadcasted_iota(jnp.int32, (rows, rows), 1)
@@ -321,12 +417,20 @@
         lambda r: lax.rem(r, part_z) // rows_z,
     )
 
-    def own_weights():
+    def own_copy(item):
         mine = pl.ds(pl.multiple_of(me_y * depth, depth), depth)
-        for item in range(items):
-            item_ref(item)[mine, :] = own_ref(item)[...]
+        return pltpu.make_async_copy(own_ref(item), item_ref(item).at[mine], own_sem.at[item])
+
+    def normalize():
+        inputs[0].wait()
+        values = tokens[...].astype(jnp.float32).reshape(samples, rows, features)
+        center = jnp.mean(values, axis=-1, keepdims=True)
+        spread = jnp.mean((values - center) ** 2, axis=-1, keepdims=True)
+        lines[0, me_z] = ((values - center) * lax.rsqrt(spread + 1e-05)).astype(jnp.bfloat16)
 
     def bias_tables():
+        for copy in inputs[1:]:
+            copy.wait()
         padded[...] = jnp.zeros(padded.shape, jnp.float32)
         for axis, table in enumerate((bias_x, bias_y, bias_z)):
             padded[axis, :, : table.shape[1]] = table[...]
@@ -346,14 +450,13 @@
 
         lax.fori_loop(0, 2 * pairs, fill, 0)
 
-    def project(group, chunk, where):
+    def project(group, chosen, where):
         blocks = pl.ds(pl.multiple_of(where * 2, 2), 2)
         flat = lines[group, blocks].reshape(2 * samples * rows, features)
-        both = jnp.concatenate([wq[2 * chunk], wq[2 * chunk + 1]], axis=1)
-        product = jnp.dot(flat, both, preferred_element_type=jnp.float32)
-        for half in range(2):
-            item = 2 * chunk + half
-            piece = product[:, half * wide : (half + 1) * wide]
+        right = jnp.concatenate([wq[item] for item in chosen], axis=1)
+        product = jnp.dot(flat, right, preferred_element_type=jnp.float32)
+        for place, item in enumerate(chosen):
+            piece = product[:, place * wide : (place + 1) * wide]
             if item % 3 == 0:
                 piece = piece * HEAD ** (-0.5)
             qkv[group, item, blocks] = piece.astype(jnp.bfloat16).reshape(2, samples, rows, wide)
@@ -385,7 +488,7 @@
             for block in range(len(blocks))
         ]
 
-    def along_x(pair):
+    def along_x(pair, where):
         def body(block, carry):
             blocks = [
                 [qkv[0, pair * 3 + m, block, sample] for m in range(3)] for sample in range(samples)
@@ -394,7 +497,7 @@
                 mixed[0, pair, block, sample] = out
             return carry
 
-        lax.fori_loop(0, size_z, body, 0)
+        lax.fori_loop(where * 2, where * 2 + 2, body, 0)
 
     def along_z(pair):
         def body(index, carry):
@@ -415,7 +518,7 @@
 
         lax.fori_loop(0, size_z, body, 0)
 
-    def along_y(pair):
+    def along_y(pair, where):
         def body(block, carry):
             blocks = [
                 [qkv[1, pair * 3 + m, block, sample] for m in range(3)] for sample in range(samples)
@@ -425,9 +528,9 @@
                     ymixed[pair, y, block * samples + sample] = out[y * part_y : (y + 1) * part_y]
             return carry
 
-        lax.fori_loop(0, size_z, body, 0)
-
-    def add_up(pair):
+        lax.fori_loop(where * 2, where * 2 + 2, body, 0)
+
+    def add_up(pair, where):
         def body(block, carry):
             for sample in range(samples):
                 there = jnp.concatenate(
@@ -438,17 +541,20 @@
                 summed[pair, block, sample] = value.astype(jnp.bfloat16)
             return carry
 
-        for copy in returns(pair):
+        for copy in returns(pair, where):
             copy.wait_recv()
-        back[pair, me_y] = ymixed[pair, me_y]
-        lax.fori_loop(0, size_z, body, 0)
-        for copy in sums_out(pair):
+        some = pl.ds(pl.multiple_of(where * 2 * samples, 2 * samples), 2 * samples)
+        back[pair, me_y, some] = ymixed[pair, me_y, some]
+        lax.fori_loop(where * 2, where * 2 + 2, body, 0)
+        for copy in sums_out(pair, where):
             copy.start()
-        parts[pair, me_z] = summed[pair, me_z]
+        if where is flank:
+            parts[pair, me_z] = summed[pair, me_z]
 
     def output(pair):
-        for copy in sums_out(pair):
-            copy.wait_recv()
+        for where in (1 - flank, flank):
+            for copy in sums_out(pair, where):
+                copy.wait_recv()
         left = jnp.concatenate(
             [parts[pair, z].reshape(samples * rows, wide) for z in range(size_z)], axis=1
         )
@@ -473,95 +579,135 @@
             if pair < pairs - 1:
                 total[:, cols] = product
             else:
-                residual = tokens[:, :, cols].astype(jnp.float32)
+                residual = tokens[:, :, :, cols].astype(jnp.float32).reshape(samples, rows, 2 * wide)
                 result[:, :, cols] = (residual + product.reshape(residual.shape)).astype(jnp.bfloat16)
 
-    early = 4
-    for item in range(early):
-        own_blocks(item)
+    other = 1 - flank
+    straight = (0, 1, 2)
+    own_rows = pl.ds(pl.multiple_of(me_y * part_y, part_y), part_y)
+    hops = levels - 1
+    order = [4, 2, 6, 3, 5, 1, 7]
+
+    def waves(first, last):
+        return [
+            [(wave - step, step) for step in range(hops) if first <= wave - step < last]
+            for wave in range(first, last + hops - 1)
+        ]
+
+    def run(wave):
+        for item, step in wave:
+            chain(item, step)
+
+    for item in straight:
+        direct(item)
+    for item in range(items):
+        own_copy(item).start()
+    normalize()
     for sample in range(samples):
         spread_piece(sample)
-    own_weights()
-    lines[1, me_z, :, pl.ds(pl.multiple_of(me_y * part_y, part_y), part_y), :] = lines[
-        0, me_z, :, pl.ds(pl.multiple_of(me_y * part_y, part_y), part_y), :
-    ]
+    lines[1, me_z, :, own_rows, :] = lines[0, me_z, :, own_rows, :]
+    for dist in (1, 2):
+        for item in straight:
+            arrive(item, dist)
     bias_tables()
-    chains(0, early)
-    for step in range(1, size_y):
+    for item in straight:
+        arrive(item, 3)
+    for step in order[:3]:
+        exchange(step).start()
+    from_side(0)
+    for step in order[3:]:
         exchange(step).start()
     spread_piece(samples)
-    for item in range(early, items):
+    for item in range(3, 6):
         own_blocks(item)
+    for item in range(items):
+        own_copy(item).wait()
     pass_on(0)
-    for item in range(2):
+    for item in range(1, 3):
         from_side(item)
     for sample in range(samples):
         to_twin(sample, twin).wait_recv()
-    project(0, 0, flank)
-    for item in range(2, 4):
-        from_side(item)
-    project(0, 1, flank)
+    project(0, (0, 1, 2), flank)
+    exchange_in(order[0])
     pass_on(1)
-    for step in range(1, 4):
-        exchange_in(step)
+    along_x(0, flank)
+    exchange_in(order[1])
+    exchange_in(order[2])
     for sample in range(samples):
         relay(sample).wait_recv()
-    project(0, 0, 1 - flank)
-    project(0, 1, 1 - flank)
-    along_x(0)
-    for step in range(4, size_y):
-        exchange_in(step)
-    chains(early, items)
+    project(0, (0, 1, 2), other)
+    exchange_in(order[3])
+    for item in range(6, 8):
+        own_blocks(item)
+    wave = waves(3, 8)
+    run(wave[0])
+    along_x(0, other)
+    exchange_in(order[4])
+    exchange_in(order[5])
+    run(wave[1])
     along_z(0)
-    for step in range(size_y):
+    exchange_in(order[6])
+    run(wave[2])
+    pass_on(samples)
+    for step in order[:2]:
         pass_on(samples + step)
     for step in range(size_y):
         to_twin(samples + step, twin).wait_recv()
-    for item in range(slots, items):
-        from_side(item)
-    share_out(0, me_z, far).start()
-    share_out(1, me_z, twin).start()
-    project(1, 0, flank)
-    project(1, 1, flank)
+    project(1, (0, 1, 2), flank)
+    run(wave[3])
+    give_back(0, flank)
+    run(wave[4])
+    for step in order[2:]:
+        pass_on(samples + step)
     for step in range(size_y):
         relay(samples + step).wait_recv()
-    project(1, 0, 1 - flank)
-    project(1, 1, 1 - flank)
-    along_y(0)
-    for copy in returns(0):
-        copy.start()
-    for item in range(early, slots):
+    project(1, (0, 1, 2), other)
+    give_back(0, other)
+    run(wave[5])
+    for item in range(3, 6):
         from_side(item)
-    project(1, 2, flank)
-    project(1, 2, 1 - flank)
-    along_y(1)
-    for copy in returns(1):
-        copy.start()
-    project(0, 2, flank)
-    project(0, 2, 1 - flank)
-    along_x(1)
-    add_up(0)
+    project(1, (3, 4, 5), other)
+    give_back(1, other)
+    run(wave[6])
+    project(1, (3, 4, 5), flank)
+    give_back(1, flank)
+    share(0)
+    project(0, (3, 4, 5), other)
+    share(1)
+    project(0, (3, 4, 5), flank)
+    add_up(0, other)
+    add_up(0, flank)
+    along_x(1, other)
     along_z(1)
-    share_out(0, far, far).wait_recv()
-    share_out(2, far, twin).start()
-    add_up(1)
-    share_out(1, twin, twin).wait_recv()
-    share_out(2, 0, twin).wait_recv()
+    add_up(1, other)
+    along_x(1, flank)
+    add_up(1, flank)
+    relay_share(0)
+    relay_share(1)
+    shared(0)
+    shared(1)
     output(0)
     output(1)
     for item in range(items):
-        drain(item)
+        if item in straight:
+            drain_direct(item)
+        else:
+            drain(item)
     for index in range(pieces):
         to_far(index).wait_send()
         to_twin(index).wait_send()
         relay(index).wait_send()
     for step in range(1, size_y):
         exchange(step).wait_send()
-    for slot in range(3):
-        share_out(slot, me_z, twin).wait_send()
+    for part in range(pairs):
+        for slot in range(2):
+            share_out(slot, part, me_z).wait_send()
+        for index in range(size_y):
+            far_block(slots + part, 0, index, me_z).wait_send()
     for pair in range(pairs):
-        for copy in returns(pair) + sums_out(pair):
-            copy.wait_send()
+        for where in (other, flank):
+            for copy in returns(pair, where) + sums_out(pair, where):
+                copy.wait_send()
 
 
 VMEM = pl.BlockSpec(memory_space=pltpu.VMEM)
@@ -579,15 +725,22 @@
     lengths = [(table.shape[1] + 1) // 2 for table in (bias_x, bias_y, bias_z)]
     width = -(-max(2 * length - 1 for length in lengths) // 128) * 128
     lookup = offset_lookup(line_places(rows, size_y, size_z, rows_z), lengths, rows, width)
+    given = (samples, depth, rows_z, features)
     block = (samples, rows, features)
     piled = (pairs, size_z, samples, rows, wide)
     sliced = (pairs, size_y, size_z * samples, rows // size_y, wide)
     result = pl.pallas_call(
-        functools.partial(heads_kernel, size_y, size_z, rows_z),
+        functools.partial(heads_kernel, size_y, size_z),
         out_shape=jax.ShapeDtypeStruct(block, jnp.bfloat16),
-        in_specs=[VMEM] * 7,
+        in_specs=[pl.BlockSpec(memory_space=pl.ANY)] * 7,
         out_specs=VMEM,
         scratch_shapes=[
+            pltpu.VMEM(given, jnp.bfloat16),
+            pltpu.VMEM(bias_x.shape, jnp.float32),
+            pltpu.VMEM(bias_y.shape, jnp.float32),
+            pltpu.VMEM(bias_z.shape, jnp.float32),
+            pltpu.VMEM(lookup.shape, jnp.float32),
+            DMA((5,)), DMA((items,)),
             pltpu.VMEM((2, size_z) + block, jnp.bfloat16),
             pltpu.VMEM((3 * pairs, features, wide), jnp.bfloat16),
             pltpu.VMEM((features // wide, features, wide), jnp.bfloat16),
@@ -605,11 +758,12 @@
         + [DMA((items, levels))] * 6
         + [DMA((size_y - 1,))] * 2
         + [DMA((pieces,))] * 6
-        + [DMA((3,))] * 2
-        + [DMA((pairs, size_y - 1))] * 2
+        + [DMA((2, pairs))] * 2
+        + [DMA((pairs, size_y))] * 2
+        + [DMA((pairs, 2, size_y - 1))] * 2
         + [DMA((pairs, size_z - 1))] * 2,
         compiler_params=pltpu.CompilerParams(collective_id=0, has_side_effects=True),
-    )(tokens.reshape(block), w_qkv, w_out, bias_x, bias_y, bias_z, jnp.asarray(lookup))
+    )(tokens.reshape(given), w_qkv, w_out, bias_x, bias_y, bias_z, jnp.asarray(lookup))
     return result.reshape(tokens.shape)
 
 
@@ -617,7 +771,7 @@
     def body(tokens, *parameters):
         _, depth, rows_y, rows_z, features = tokens.shape
         rows = depth * rows_y * rows_z
-        fits = size_y % 2 == 0 and size_z == 4 and HEADS % (4 * size_z) == 0 and rows == 2 * HEAD
+        fits = size_y == 8 and size_z == 4 and HEADS % (4 * size_z) == 0 and rows == 2 * HEAD
         if fits and rows_y == 1 and rows % (16 * size_y) == 0 and rows % (16 * size_z) == 0:
             return fast_shards(size_y, size_z, tokens, *parameters)
         return shards(tokens, *parameters)

time: 68.1 us -> 65.9 us (0.968); the launches traced: 67.1 us -> 65.7 us
  local copies, waits for them, and re-layouts: 4.07 us -> 2.03 us
  Pallas kernels: 63 us -> 63.7 us
    reshape x1 -> x0, local copies, waits for them, and re-layouts: 2.03 us -> none  [fast_shards(): tokens.reshape(block)]
where the time goes in v2:
time: 65.9 us; the launch traced here: 65.7 us
  Pallas kernels  63.7 us (97%)
  local copies, waits for them, and re-layouts  2.03 us (3%)
    pallas_call x1, Pallas kernels, fast_shards(): pl.pallas_call(functools.partial(heads_kernel, size_y, size_z), out_shape...  63.7 us
    reshape x1, local copies, waits for them, and re-layouts, fast_shards(): return result.reshape(tokens.shape)  2.03 us

profile of v2, /device:TPU:1, one launch (start us, length us, event | category | flops | bytes accessed | tf_op | source)
XLA Modules:
  0.0 65.7 jit_solution(13039033869566067334)
XLA Ops:
  0.0 63.7 %shard_map.73 = bf16[2,128,1024]{2,1,0:T(8,128)(2,1)} custom-call(bf16[2,64,2,1024]{3,2,1,0:T(2,128)(2,1)} %bitcast.2, bf16[128,3072]{1,0:T(8,128)(2,1)} %w_qkv.1, bf16[128,1024]{1,0:T(8,128)(2,1)} %w_out.1, f32[16,127]{1,0:T(8,128)} %bias_x_in.1, f32[16,15]{1,0:T(8,128)} %bias_y_in.1, f32[16,15]{1,0:T(8,128)} %bias_z_in.1, ...), custom_call_target="tpu_custom_call" | custom-call | tf_op jit(solution)/shard_map/pallas_call | solution.py:732
  63.7 2.0 %reshape.7 = bf16[2,64,1,2,1024]{4,3,1,0,2:T(2,128)(2,1)} reshape(bf16[2,128,1024]{2,1,0:T(8,128)(2,1)} %shard_map.73) | data formatting | bytes 1048576 | tf_op jit(solution)/shard_map/reshape | solution.py:767

commit v3 on v2

--- a/solution.py
+++ b/solution.py
@@ -213,21 +213,19 @@
     def across_in(item, lev):
         return transfer(item, lev, 1 - side, side_send, side_recv, lev, beside)
 
-    def far_block(item, lev, sid, gz, own=False):
+    def far_block(item, lev, sid, gz):
         part, index = item - slots, lev * 2 + sid
         ref = wo.at[gz * pairs + part].at[pl.ds(pl.multiple_of(index * depth, depth), depth)]
-        source = own_ref(item) if own else ref
-        return remote(source, ref, of_send.at[part, index], of_recv.at[part, index], gz=far)
-
-    def block_out(item, lev, sid, own=False):
+        return remote(ref, ref, of_send.at[part, index], of_recv.at[part, index], gz=far)
+
+    def block_out(item, lev, sid):
         if item >= slots:
-            far_block(item, lev, sid, me_z, own).start()
+            far_block(item, lev, sid, me_z).start()
 
     def own_blocks(item):
         pl.when(level + 1 < levels)(lambda: up(item, 0, True).start())
         pl.when(level > 0)(lambda: down(item, 0, True).start())
         across(item, level, True).start()
-        block_out(item, level, side, True)
 
     def chain(item, step):
         @pl.when(level - 1 - step >= 0)
@@ -258,7 +256,6 @@
         for dist in (1, 2):
             pl.when(level + dist < levels)(lambda: reach(item, dist, True).start())
             pl.when(level - dist >= 0)(lambda: reach(item, dist, False).start())
-        block_out(item, level, side, True)
 
     def arrive(item, dist):
         @pl.when(level - dist >= 0)
@@ -371,7 +368,7 @@
 
     def relay_share(part):
         for index in range(size_y):
-            far_block(slots + part, 0, index, far).wait_recv()
+            pl.when(index != me_y)(lambda: far_block(slots + part, 0, index, far).wait_recv())
         share_out(1, part, far).start()
 
     def shared(part):
@@ -419,6 +416,10 @@
 
     def own_copy(item):
         mine = pl.ds(pl.multiple_of(me_y * depth, depth), depth)
+        if item >= items:
+            block = far * pairs + item - items
+            source = w_out.at[:, pl.ds(pl.multiple_of(block * wide, wide), wide)]
+            return pltpu.make_async_copy(source, wo.at[block].at[mine], own_sem.at[item])
         return pltpu.make_async_copy(own_ref(item), item_ref(item).at[mine], own_sem.at[item])
 
     def normalize():
@@ -583,107 +584,95 @@
                 result[:, :, cols] = (residual + product.reshape(residual.shape)).astype(jnp.bfloat16)
 
     other = 1 - flank
-    straight = (0, 1, 2)
+    straight = ()
     own_rows = pl.ds(pl.multiple_of(me_y * part_y, part_y), part_y)
     hops = levels - 1
     order = [4, 2, 6, 3, 5, 1, 7]
 
-    def waves(first, last):
-        return [
-            [(wave - step, step) for step in range(hops) if first <= wave - step < last]
-            for wave in range(first, last + hops - 1)
-        ]
-
-    def run(wave):
-        for item, step in wave:
-            chain(item, step)
-
-    for item in straight:
-        direct(item)
-    for item in range(items):
+    def run(first, last, *turns):
+        for turn in turns:
+            for step in range(hops):
+                if first <= turn - step < last:
+                    chain(turn - step, step)
+
+    for item in range(slots):
+        own_blocks(item)
+    for item in range(items + pairs):
         own_copy(item).start()
     normalize()
     for sample in range(samples):
         spread_piece(sample)
     lines[1, me_z, :, own_rows, :] = lines[0, me_z, :, own_rows, :]
-    for dist in (1, 2):
-        for item in straight:
-            arrive(item, dist)
     bias_tables()
-    for item in straight:
-        arrive(item, 3)
+    run(0, slots, 0, 1, 2, 3)
+    pass_on(0)
+    run(0, slots, 4, 5)
+    pass_on(1)
+    run(0, slots, 6)
     for step in order[:3]:
         exchange(step).start()
+    run(0, slots, 7)
     from_side(0)
     for step in order[3:]:
         exchange(step).start()
     spread_piece(samples)
-    for item in range(3, 6):
+    for item in range(slots, items):
         own_blocks(item)
-    for item in range(items):
+    for item in range(items + pairs):
         own_copy(item).wait()
-    pass_on(0)
     for item in range(1, 3):
         from_side(item)
     for sample in range(samples):
         to_twin(sample, twin).wait_recv()
+        relay(sample).wait_recv()
     project(0, (0, 1, 2), flank)
     exchange_in(order[0])
-    pass_on(1)
+    project(0, (0, 1, 2), other)
+    exchange_in(order[1])
     along_x(0, flank)
-    exchange_in(order[1])
     exchange_in(order[2])
-    for sample in range(samples):
-        relay(sample).wait_recv()
-    project(0, (0, 1, 2), other)
+    along_x(0, other)
     exchange_in(order[3])
-    for item in range(6, 8):
-        own_blocks(item)
-    wave = waves(3, 8)
-    run(wave[0])
-    along_x(0, other)
+    run(slots, items, slots)
+    along_z(0)
     exchange_in(order[4])
     exchange_in(order[5])
-    run(wave[1])
-    along_z(0)
+    for item in range(3, 6):
+        from_side(item)
+    run(slots, items, slots + 1)
+    project(0, (3, 4, 5), flank)
     exchange_in(order[6])
-    run(wave[2])
+    run(slots, items, slots + 2)
     pass_on(samples)
-    for step in order[:2]:
+    for step in order[:3]:
         pass_on(samples + step)
     for step in range(size_y):
         to_twin(samples + step, twin).wait_recv()
     project(1, (0, 1, 2), flank)
-    run(wave[3])
+    run(slots, items, slots + 3)
     give_back(0, flank)
-    run(wave[4])
-    for step in order[2:]:
+    share(0)
+    project(1, (3, 4, 5), flank)
+    give_back(1, flank)
+    share(1)
+    for step in order[3:]:
         pass_on(samples + step)
     for step in range(size_y):
         relay(samples + step).wait_recv()
     project(1, (0, 1, 2), other)
     give_back(0, other)
-    run(wave[5])
-    for item in range(3, 6):
-        from_side(item)
     project(1, (3, 4, 5), other)
     give_back(1, other)
-    run(wave[6])
-    project(1, (3, 4, 5), flank)
-    give_back(1, flank)
-    share(0)
     project(0, (3, 4, 5), other)
-    share(1)
-    project(0, (3, 4, 5), flank)
+    add_up(0, flank)
     add_up(0, other)
-    add_up(0, flank)
+    relay_share(0)
     along_x(1, other)
+    relay_share(1)
     along_z(1)
     add_up(1, other)
     along_x(1, flank)
     add_up(1, flank)
-    relay_share(0)
-    relay_share(1)
     shared(0)
     shared(1)
     output(0)
@@ -703,7 +692,7 @@
         for slot in range(2):
             share_out(slot, part, me_z).wait_send()
         for index in range(size_y):
-            far_block(slots + part, 0, index, me_z).wait_send()
+            pl.when(index != me_y)(lambda: far_block(slots + part, 0, index, me_z).wait_send())
     for pair in range(pairs):
         for where in (other, flank):
             for copy in returns(pair, where) + sums_out(pair, where):
@@ -740,7 +729,7 @@
             pltpu.VMEM(bias_y.shape, jnp.float32),
             pltpu.VMEM(bias_z.shape, jnp.float32),
             pltpu.VMEM(lookup.shape, jnp.float32),
-            DMA((5,)), DMA((items,)),
+            DMA((5,)), DMA((items + pairs,)),
             pltpu.VMEM((2, size_z) + block, jnp.bfloat16),
             pltpu.VMEM((3 * pairs, features, wide), jnp.bfloat16),
             pltpu.VMEM((features // wide, features, wide), jnp.bfloat16),

time: 65.9 us -> 64.4 us (0.977); the launches traced: 65.7 us -> 63.5 us
  Pallas kernels: 63.7 us -> 61.5 us
    pallas_call x1, Pallas kernels: 63.7 us -> 61.5 us  [fast_shards(): pl.pallas_call(functools.partial(heads_kernel, size_y, size_z), out_shape...]
where the time goes in v3:
time: 64.4 us; the launch traced here: 63.5 us
  Pallas kernels  61.5 us (95%)
  local copies, waits for them, and re-layouts  2.03 us (3%)
    pallas_call x1, Pallas kernels, fast_shards(): pl.pallas_call(functools.partial(heads_kernel, size_y, size_z), out_shape...  61.5 us
    reshape x1, local copies, waits for them, and re-layouts, fast_shards(): return result.reshape(tokens.shape)  2.03 us

profile of v3, /device:TPU:1, one launch (start us, length us, event | category | flops | bytes accessed | tf_op | source)
XLA Modules:
  0.0 63.5 jit_solution(6527046313404687637)
XLA Ops:
  0.0 61.5 %shard_map.73 = bf16[2,128,1024]{2,1,0:T(8,128)(2,1)} custom-call(bf16[2,64,2,1024]{3,2,1,0:T(2,128)(2,1)} %bitcast.2, bf16[128,3072]{1,0:T(8,128)(2,1)} %w_qkv.1, bf16[128,1024]{1,0:T(8,128)(2,1)} %w_out.1, f32[16,127]{1,0:T(8,128)} %bias_x_in.1, f32[16,15]{1,0:T(8,128)} %bias_y_in.1, f32[16,15]{1,0:T(8,128)} %bias_z_in.1, ...), custom_call_target="tpu_custom_call" | custom-call | tf_op jit(solution)/shard_map/pallas_call | solution.py:721
  61.5 2.0 %reshape.7 = bf16[2,64,1,2,1024]{4,3,1,0,2:T(2,128)(2,1)} reshape(bf16[2,128,1024]{2,1,0:T(8,128)(2,1)} %shard_map.73) | data formatting | bytes 1048576 | tf_op jit(solution)/shard_map/reshape | solution.py:756

commit v4 on v3

--- a/solution.py
+++ b/solution.py
@@ -218,10 +218,6 @@
         ref = wo.at[gz * pairs + part].at[pl.ds(pl.multiple_of(index * depth, depth), depth)]
         return remote(ref, ref, of_send.at[part, index], of_recv.at[part, index], gz=far)
 
-    def block_out(item, lev, sid):
-        if item >= slots:
-            far_block(item, lev, sid, me_z).start()
-
     def own_blocks(item):
         pl.when(level + 1 < levels)(lambda: up(item, 0, True).start())
         pl.when(level > 0)(lambda: down(item, 0, True).start())
@@ -233,14 +229,12 @@
             up_in(item, step).wait_recv()
             pl.when(level + 1 < levels)(lambda: up(item, step + 1).start())
             across(item, level - 1 - step).start()
-            block_out(item, level - 1 - step, side)
 
         @pl.when(level + 1 + step < levels)
         def _():
             down_in(item, step).wait_recv()
             pl.when(level > 0)(lambda: down(item, step + 1).start())
             across(item, level + 1 + step).start()
-            block_out(item, level + 1 + step, side)
 
     def reach(item, dist, rise, passed=False):
         sends, recvs = (up_send, up_recv) if rise else (down_send, down_recv)
@@ -264,7 +258,6 @@
             if dist == 2:
                 pl.when(level + 1 < levels)(lambda: reach(item, 3, True, True).start())
             across(item, level - dist).start()
-            block_out(item, level - dist, side)
 
         @pl.when(level + dist < levels)
         def _():
@@ -272,7 +265,6 @@
             if dist == 2:
                 pl.when(level > 0)(lambda: reach(item, 3, False, True).start())
             across(item, level + dist).start()
-            block_out(item, level + dist, side)
 
     def drain_direct(item):
         across(item, level, True).wait_send()
@@ -300,7 +292,6 @@
     def from_side(item):
         for lev in range(levels):
             across_in(item, lev).wait_recv()
-            block_out(item, lev, 1 - side)
 
     def drain(item):
         pl.when(level + 1 < levels)(lambda: up(item, 0, True).wait_send())
@@ -364,6 +355,8 @@
 
     def share(part):
         from_side(slots + part)
+        for index in range(size_y):
+            pl.when(index != me_y)(lambda: far_block(slots + part, 0, index, me_z).start())
         share_out(0, part, me_z).start()
 
     def relay_share(part):
@@ -612,12 +605,12 @@
     for step in order[:3]:
         exchange(step).start()
     run(0, slots, 7)
+    for item in range(slots, items):
+        own_blocks(item)
     from_side(0)
     for step in order[3:]:
         exchange(step).start()
     spread_piece(samples)
-    for item in range(slots, items):
-        own_blocks(item)
     for item in range(items + pairs):
         own_copy(item).wait()
     for item in range(1, 3):
@@ -651,12 +644,12 @@
     project(1, (0, 1, 2), flank)
     run(slots, items, slots + 3)
     give_back(0, flank)
+    for step in order[3:]:
+        pass_on(samples + step)
     share(0)
     project(1, (3, 4, 5), flank)
     give_back(1, flank)
     share(1)
-    for step in order[3:]:
-        pass_on(samples + step)
     for step in range(size_y):
         relay(samples + step).wait_recv()
     project(1, (0, 1, 2), other)
@@ -664,14 +657,14 @@
     project(1, (3, 4, 5), other)
     give_back(1, other)
     project(0, (3, 4, 5), other)
+    along_x(1, other)
     add_up(0, flank)
+    along_z(1)
     add_up(0, other)
     relay_share(0)
-    along_x(1, other)
-    relay_share(1)
-    along_z(1)
     add_up(1, other)
     along_x(1, flank)
+    relay_share(1)
     add_up(1, flank)
     shared(0)
     shared(1)

time: 64.4 us -> 62.2 us (0.966); the launches traced: 63.5 us -> 62 us
  Pallas kernels: 61.5 us -> 60 us
    pallas_call x1, Pallas kernels: 61.5 us -> 60 us  [fast_shards(): pl.pallas_call(functools.partial(heads_kernel, size_y, size_z), out_shape...]
where the time goes in v4:
time: 62.2 us; the launch traced here: 62 us
  Pallas kernels  60 us (96%)
  local copies, waits for them, and re-layouts  2.03 us (3%)
    pallas_call x1, Pallas kernels, fast_shards(): pl.pallas_call(functools.partial(heads_kernel, size_y, size_z), out_shape...  60 us
    reshape x1, local copies, waits for them, and re-layouts, fast_shards(): return result.reshape(tokens.shape)  2.03 us

profile of v4, /device:TPU:1, one launch (start us, length us, event | category | flops | bytes accessed | tf_op | source)
XLA Modules:
  0.0 62.0 jit_solution(13497744730567434208)
XLA Ops:
  0.0 60.0 %shard_map.73 = bf16[2,128,1024]{2,1,0:T(8,128)(2,1)} custom-call(bf16[2,64,2,1024]{3,2,1,0:T(2,128)(2,1)} %bitcast.2, bf16[128,3072]{1,0:T(8,128)(2,1)} %w_qkv.1, bf16[128,1024]{1,0:T(8,128)(2,1)} %w_out.1, f32[16,127]{1,0:T(8,128)} %bias_x_in.1, f32[16,15]{1,0:T(8,128)} %bias_y_in.1, f32[16,15]{1,0:T(8,128)} %bias_z_in.1, ...), custom_call_target="tpu_custom_call" | custom-call | tf_op jit(solution)/shard_map/pallas_call | solution.py:714
  60.0 2.0 %reshape.7 = bf16[2,64,1,2,1024]{4,3,1,0,2:T(2,128)(2,1)} reshape(bf16[2,128,1024]{2,1,0:T(8,128)(2,1)} %shard_map.73) | data formatting | bytes 1048576 | tf_op jit(solution)/shard_map/reshape | solution.py:749

commit v5 on v4

--- a/solution.py
+++ b/solution.py
@@ -167,7 +167,7 @@
         copy.start()
 
     barrier = pltpu.get_barrier_semaphore()
-    for dist in (1, 2):
+    for dist in (1,):
         pl.when(level + dist < levels)(
             lambda: pl.semaphore_signal(barrier, inc=1, **device(gy=me_y + 2 * dist))
         )
@@ -177,7 +177,7 @@
     pl.semaphore_signal(barrier, inc=1, **device(**beside))
     pl.semaphore_signal(barrier, inc=1, **device(gz=twin))
     pl.semaphore_signal(barrier, inc=1, **device(gz=far))
-    near = jnp.minimum(level, 2) + jnp.minimum(levels - 1 - level, 2)
+    near = jnp.minimum(level, 1) + jnp.minimum(levels - 1 - level, 1)
     pl.semaphore_wait(barrier, near + 3)
 
     def item_ref(item):
@@ -663,8 +663,8 @@
     add_up(0, other)
     relay_share(0)
     add_up(1, other)
+    relay_share(1)
     along_x(1, flank)
-    relay_share(1)
     add_up(1, flank)
     shared(0)
     shared(1)

time: 62.2 us -> 61.7 us (level)
  no operation moved by 1% of the time
where the time goes in v5:
time: 61.7 us; the launch traced here: 61.5 us
  Pallas kernels  59.5 us (96%)
  local copies, waits for them, and re-layouts  2.03 us (3%)
    pallas_call x1, Pallas kernels, fast_shards(): pl.pallas_call(functools.partial(heads_kernel, size_y, size_z), out_shape...  59.5 us
    reshape x1, local copies, waits for them, and re-layouts, fast_shards(): return result.reshape(tokens.shape)  2.03 us

profile of v5, /device:TPU:1, one launch (start us, length us, event | category | flops | bytes accessed | tf_op | source)
XLA Modules:
  0.0 61.5 jit_solution(7328102930934254314)
XLA Ops:
  0.0 59.5 %shard_map.73 = bf16[2,128,1024]{2,1,0:T(8,128)(2,1)} custom-call(bf16[2,64,2,1024]{3,2,1,0:T(2,128)(2,1)} %bitcast.2, bf16[128,3072]{1,0:T(8,128)(2,1)} %w_qkv.1, bf16[128,1024]{1,0:T(8,128)(2,1)} %w_out.1, f32[16,127]{1,0:T(8,128)} %bias_x_in.1, f32[16,15]{1,0:T(8,128)} %bias_y_in.1, f32[16,15]{1,0:T(8,128)} %bias_z_in.1, ...), custom_call_target="tpu_custom_call" | custom-call | tf_op jit(solution)/shard_map/pallas_call | solution.py:714
  59.5 2.0 %reshape.7 = bf16[2,64,1,2,1024]{4,3,1,0,2:T(2,128)(2,1)} reshape(bf16[2,128,1024]{2,1,0:T(8,128)(2,1)} %shard_map.73) | data formatting | bytes 1048576 | tf_op jit(solution)/shard_map/reshape | solution.py:749
